TPU v7x, 32 devices: a whole 2x2x4 slice. The times are simulated.
32 devices in a mesh: group: 4 (over y, x), dp: 8 (over z, core).
Axes of the slice: x: 2, y: 2, z: 4, core: 2. Of those that a mesh axis runs over, the one named last changes fastest.
Arguments:
- observations: bfloat16 [64, 64, 4096], P('dp', None, 'group'), may hold values from -6 to 6
- next_observations: bfloat16 [1024, 4096], P('dp', 'group'), may hold values from -6 to 6
- trunk_weights: bfloat16 [2, 4096, 4096], P(None, 'dp', 'group'), may hold values from -0.125 to 0.125
- head_weights: bfloat16 [4096, 19], P('group'), may hold values from -0.25 to 0.25
- acting_policy_logits: float32 [64, 63, 18], P('dp'), may hold values from -16 to 330, as said below
- actions: int32 [64, 63], P('dp'), may hold values from 0 to 17
- rewards: float32 [64, 63], P('dp'), may hold values from -6 to 6
- episode_finished: int32 [64, 63], P('dp'), may hold values 0 or 1
Outputs:
- trunk_grads: float32 [2, 4096, 4096], P(None, 'dp', 'group')
- head_grads: float32 [4096, 19], P(('group', 'dp'))
- actor_logits: float32 [1024, 18], P('dp')
Inputs may be any that keep to these rules, and one draw needn't show every extreme that they name: `acting_policy_logits`: Real-valued scores, one row for each step and trajectory.
All inputs are finite; a program needn't handle non-finite values. No bound on the sum of `episode_finished` on one device may be relied on, other than what follows from the above.
Results may differ from a plain program's by a relative error of at most 0.012.
Values may be sent and summed in bfloat16 or wider, within the bound.
A program may use at most 128 MiB of HBM per device.

v0:
```python
import jax
import jax.numpy as jnp
from jax import lax
from jax.sharding import PartitionSpec as P

discount_rate = 0.99
value_weight = 0.5
entropy_weight = 0.1
loss_divisor = 16.0


def contract_rows(left, right):
    return lax.dot_general(
        left, right, (((0,), (0,)), ((), ())), preferred_element_type=jnp.float32
    )


def contract_cols(left, right):
    return lax.dot_general(
        left, right, (((1,), (1,)), ((), ())), preferred_element_type=jnp.float32
    )


def silu_slope(pre_value):
    sigma = jax.nn.sigmoid(pre_value)
    return sigma * (1.0 + pre_value * (1.0 - sigma))


def importance_trace_gradients(
    learner_output, acting_policy_logits, actions, rewards, episode_finished
):
    number_of_actions = acting_policy_logits.shape[-1]
    logits = learner_output[:, :, :number_of_actions]
    values = learner_output[:, :, number_of_actions]
    log_policy = jax.nn.log_softmax(logits[:, :-1], axis=-1)
    log_behave = jax.nn.log_softmax(acting_policy_logits, axis=-1)
    chosen = (
        actions[:, :, None] == jnp.arange(number_of_actions, dtype=jnp.int32)[None, None, :]
    ).astype(jnp.float32)
    ratio = jnp.exp(jnp.sum((log_policy - log_behave) * chosen, axis=-1))
    clipped = jnp.minimum(ratio, 1.0)
    discount = discount_rate * (1.0 - episode_finished.astype(jnp.float32))
    current = values[:, :-1]
    following = values[:, 1:]
    deltas = clipped * (rewards + discount * following - current)

    def backward_step(carried, step_item):
        delta_now, factor_now = step_item
        carried = delta_now + factor_now * carried
        return (carried, carried)

    start_carry = jnp.zeros((values.shape[0],), jnp.float32)
    _, corrections = lax.scan(
        backward_step, start_carry, (deltas.T, (discount * clipped).T), reverse=True
    )
    targets = current + corrections.T
    next_targets = jnp.concatenate([targets[:, 1:], values[:, -1:]], axis=1)
    advantage = clipped * (rewards + discount * next_targets - current)
    probability = jnp.exp(log_policy)
    entropy = -jnp.sum(probability * log_policy, axis=-1)
    logit_grad = (
        -advantage[..., None] * (chosen - probability)
        + entropy_weight * probability * (log_policy + entropy[..., None])
    ) / loss_divisor
    value_grad = -value_weight * (targets - current) / loss_divisor
    step_grad = jnp.concatenate([logit_grad, value_grad[..., None]], axis=-1)
    last_row = jnp.zeros((values.shape[0], 1, number_of_actions + 1), jnp.float32)
    return jnp.concatenate([step_grad, last_row], axis=1)


def per_device(
    observations,
    next_observations,
    trunk_weights,
    head_weights,
    acting_policy_logits,
    actions,
    rewards,
    episode_finished,
):
    traj_count, step_count, feature_block = observations.shape
    learner_rows = traj_count * step_count
    number_of_actions = acting_policy_logits.shape[-1]
    layer_total = trunk_weights.shape[0]
    own_rows = observations.reshape(learner_rows, feature_block)
    gathered_weights = [
        lax.all_gather(trunk_weights[layer_index], "dp", axis=0, tiled=True)
        for layer_index in range(layer_total)
    ]
    joined = jnp.concatenate([own_rows, next_observations], axis=0)
    inputs_full = []
    products_block = []
    current = joined
    for forward_layer_index in range(layer_total):
        forward_whole = lax.all_gather(current, "group", axis=1, tiled=True)
        inputs_full.append(forward_whole)
        product = jnp.dot(
            forward_whole, gathered_weights[forward_layer_index], preferred_element_type=jnp.float32
        )
        products_block.append(product)
        current = jax.nn.silu(product).astype(jnp.bfloat16)
    partial_head = jnp.dot(current, head_weights, preferred_element_type=jnp.float32)
    totals = lax.psum(partial_head, "group")
    inputs_full, products_block, last_block, totals = (inputs_full, products_block, current, totals)
    inputs_full = [whole[:learner_rows] for whole in inputs_full]
    products_block = [block[:learner_rows] for block in products_block]
    last_block = last_block[:learner_rows]
    head_out = totals[:learner_rows]
    actor_logits = totals[learner_rows:, :number_of_actions]
    learner_output = head_out.reshape(traj_count, step_count, number_of_actions + 1)
    output_gradient = importance_trace_gradients(
        learner_output, acting_policy_logits, actions, rewards, episode_finished
    )
    output_gradient = output_gradient.reshape(learner_rows, number_of_actions + 1).astype(
        jnp.bfloat16
    )
    head_partial = contract_rows(last_block, output_gradient)
    head_grads = lax.psum_scatter(head_partial, "dp", scatter_dimension=0, tiled=True)
    input_grad = contract_cols(output_gradient, head_weights)
    grad_list = [None] * layer_total
    for layer_index in range(layer_total - 1, -1, -1):
        pre_grad = (input_grad * silu_slope(products_block[layer_index])).astype(jnp.bfloat16)
        all_inputs = lax.all_to_all(
            inputs_full[layer_index], "dp", split_axis=1, concat_axis=0, tiled=True
        )
        all_upstream = lax.all_gather(pre_grad, "dp", axis=0, tiled=True)
        grad_list[layer_index] = contract_rows(all_inputs, all_upstream)
        if layer_index > 0:
            full_grad = contract_cols(pre_grad, gathered_weights[layer_index])
            input_grad = lax.psum_scatter(full_grad, "group", scatter_dimension=1, tiled=True)
    return (jnp.stack(grad_list), head_grads, actor_logits)


def solution(mesh):
    in_specs = (
        P("dp", None, "group"),
        P("dp", "group"),
        P(None, "dp", "group"),
        P("group", None),
        P("dp", None, None),
        P("dp", None),
        P("dp", None),
        P("dp", None),
    )
    out_specs = (P(None, "dp", "group"), P(("group", "dp"), None), P("dp", None))
    return jax.shard_map(
        per_device, mesh=mesh, in_specs=in_specs, out_specs=out_specs, check_vma=False
    )
```

profile of v0, /device:TPU:0, one launch (start us, length us, event | category | flops | bytes accessed | tf_op | source)
XLA Modules:
  0.0 727.3 jit_solution(5411754395285372085)
XLA Ops:
  7.2 2.6 pad_maximum_fusion.1
  12.3 62.2 %all-gather.9.cloned.1.call-done = bf16[640,4096]{1,0:T(8,128)(2,1)} async-done(((bf16[640,1024]{1,0:T(8,128)(2,1)}), bf16[640,4096]{1,0:T(8,128)(2,1)}) %all-gather.9.cloned.1.call-update) | async-done | bytes 5242896 | tf_op jit(solution)/shard_map/all_gather | solution.py:95
  74.5 83.7 %all-gather.17.cloned.1.call-done = bf16[1,4096,1024]{2,1,0:T(8,128)(2,1)} async-done(((bf16[1,512,1024]{2,1,0:T(8,128)(2,1)}), bf16[1,4096,1024]{2,1,0:T(8,128)(2,1)}) %all-gather.17.cloned.1.call-update) | async-done | bytes 8388624 | tf_op jit(solution)/shard_map/all_gather | solution.py:87
  158.1 10.7 %multiply_convert_fusion.1 = (bf16[640,1024]{1,0:T(8,128)(2,1)}, f32[640,1024]{1,0:T(8,128)S(1)}) fusion(bf16[640,4096]{1,0:T(8,128)(2,1)} %all-gather.9.cloned.1.call-done, bf16[1,4096,1024]{2,1,0:T(8,128)(2,1)} %all-gather.17.cloned.1.call-done), kind=kOutput, calls=%fused_computation.12 | convolution fusion | flops 5371985920 | bytes 17563648 | tf_op jit(solution)/shard_map/dot_general | solution.py:97
  169.1 71.2 %all-gather.19.cloned.1.call-done = bf16[1,4096,1024]{2,1,0:T(8,128)(2,1)} async-done(((bf16[1,512,1024]{2,1,0:T(8,128)(2,1)}), bf16[1,4096,1024]{2,1,0:T(8,128)(2,1)}) %all-gather.19.cloned.1.call-update) | async-done | bytes 8388624 | tf_op jit(solution)/shard_map/all_gather | solution.py:87
  240.3 62.1 %all-gather.11.cloned.1.call-done = bf16[640,4096]{1,0:T(8,128)(2,1)} async-done(((bf16[640,1024]{1,0:T(8,128)(2,1)}), bf16[640,4096]{1,0:T(8,128)(2,1)}) %all-gather.11.cloned.1.call-update) | async-done | bytes 5242896 | tf_op jit(solution)/shard_map/all_gather | solution.py:95
  302.4 10.9 %multiply_convert_fusion = (bf16[640,1024]{1,0:T(8,128)(2,1)S(1)}, f32[640,1024]{1,0:T(8,128)}) fusion(bf16[640,4096]{1,0:T(8,128)(2,1)} %all-gather.11.cloned.1.call-done, bf16[1,4096,1024]{2,1,0:T(8,128)(2,1)} %all-gather.19.cloned.1.call-done), kind=kOutput, calls=%fused_computation.11 | convolution fusion | flops 5371985920 | bytes 17563648 | tf_op jit(solution)/shard_map/dot_general | solution.py:97
  314.8 16.2 %psum.7 = f32[640,19]{0,1:T(8,128)S(1)} all-reduce(f32[640,19]{0,1:T(8,128)S(1)} %fusion.28), channel_id=1, replica_groups=mesh['group'=4,'dp'=8] {'group'}, use_global_device_ids=true, to_apply=%region_0.1 | all-reduce | flops 12160 | bytes 97280 | tf_op jit(solution)/shard_map/psum | solution.py:103
  331.5 4.7 while.17
  336.7 3.4 multiply_convert_fusion.3
  340.1 11.5 %fusion.2 = f32[512,4096]{1,0:T(8,128)} fusion(bf16[512,1024]{1,0:T(8,128)(2,1)} %multiply_convert_fusion.3, bf16[1,4096,1024]{2,1,0:T(8,128)(2,1)} %all-gather.19.cloned.1.call-done), kind=kOutput, calls=%fused_computation.3 | convolution fusion | flops 4294967296 | bytes 17825792 | tf_op jit(solution)/shard_map/dot_general | solution.py:19
  352.3 4.7 slice.62
  357.0 6.6 copy.47
  363.6 4.6 all-to-all-start
  368.4 69.6 %reduce-scatter.3.cloned.1.call-done = f32[512,1024]{1,0:T(8,128)} async-done(((f32[512,4096]{1,0:T(8,128)}), f32[512,1024]{1,0:T(8,128)}) %reduce-scatter.3.cloned.1.call-update) | async-done | bytes 2097168 | tf_op jit(solution)/shard_map/reduce_scatter | solution.py:130
  438.0 3.3 multiply_convert_fusion.2
  445.9 50.0 %all-to-all-done = bf16[512,8,512]{0,2,1:T(8,128)(2,1)} async-done(((bf16[512,8,512]{0,2,1:T(8,128)(2,1)}), bf16[512,8,512]{0,2,1:T(8,128)(2,1)}, u32[]{:S(2)}, u32[]{:S(2)}) %all-to-all-start) | async-done | bytes 4194336 | tf_op jit(solution)/shard_map/all_to_all | solution.py:123
  495.9 4.6 all-to-all-start.1
  500.5 6.6 copy.48
  508.7 146.3 %all-to-all-done.1 = bf16[512,8,512]{2,0,1:T(8,128)(2,1)} async-done(((bf16[512,8,512]{2,0,1:T(8,128)(2,1)}), bf16[512,8,512]{2,0,1:T(8,128)(2,1)}, u32[]{:S(2)}, u32[]{:S(2)}) %all-to-all-start.1) | async-done | bytes 4194336 | tf_op jit(solution)/shard_map/all_to_all | solution.py:123
  655.0 8.3 %convolution_bitcast_fusion = f32[1,512,1024]{2,1,0:T(8,128)S(1)} fusion(bf16[4096,512]{1,0:T(8,128)(2,1)} %bitcast.13, bf16[4096,1024]{1,0:T(8,128)(2,1)} %all-gather.15.cloned.1.call-done), kind=kOutput, calls=%fused_computation.15 | convolution fusion | flops 4294967296 | bytes 14680064 | tf_op jit(solution)/shard_map/dot_general | solution.py:13
  663.3 26.0 %all-gather.13.cloned.1.call-done = bf16[4096,1024]{1,0:T(8,128)(2,1)} async-done(((bf16[512,1024]{1,0:T(8,128)(2,1)}), bf16[4096,1024]{1,0:T(8,128)(2,1)}) %all-gather.13.cloned.1.call-update) | async-done | bytes 8388624 | tf_op jit(solution)/shard_map/all_gather | solution.py:126
  689.3 8.2 %convolution_bitcast_fusion.1 = f32[1,512,1024]{2,1,0:T(8,128)S(1)} fusion(bf16[4096,512]{1,0:T(8,128)(2,1)} %bitcast.68, bf16[4096,1024]{1,0:T(8,128)(2,1)} %all-gather.13.cloned.1.call-done), kind=kOutput, calls=%fused_computation.16 | convolution fusion | flops 4294967296 | bytes 14680064 | tf_op jit(solution)/shard_map/dot_general | solution.py:13
  700.0 20.5 %reduce-scatter.5.cloned.1.call-done = f32[128,19]{0,1:T(8,128)} async-done(((f32[1024,19]{0,1:T(8,128)}), f32[128,19]{0,1:T(8,128)}) %reduce-scatter.5.cloned.1.call-update) | async-done | bytes 9744 | tf_op jit(solution)/shard_map/reduce_scatter | solution.py:118
  (193 shorter events, 18.1 us)
Async XLA Ops:
  7.2 307.2 %copy-start = (bf16[1024,19]{0,1:T(8,128)(2,1)S(1)}, bf16[1024,19]{0,1:T(8,128)(2,1)}, u32[]{:S(2)}) copy-start(bf16[1024,19]{0,1:T(8,128)(2,1)} %param.14) | copy-start | bytes 116740
  7.2 2.7 copy-start.2
  7.2 67.3 %all-gather.9.cloned.1.call-start = ((), (), s32[]{:S(2)}) async-start(), calls=%async_computation.4 | async-start | bytes 6553600 | tf_op jit(solution)/shard_map/all_gather | solution.py:95
  9.9 148.3 %all-gather.17.cloned.1.call-start = ((), (), s32[]{:S(2)}) async-start(), calls=%async_computation.10 | async-start | bytes 9437184 | tf_op jit(solution)/shard_map/all_gather | solution.py:87
  11.5 228.8 %all-gather.19.cloned.1.call-start = ((), (), s32[]{:S(2)}) async-start(), calls=%async_computation.11 | async-start | bytes 9437184 | tf_op jit(solution)/shard_map/all_gather | solution.py:87
  12.2 156.8 %copy-start.5 = (f32[8,63,18]{1,0,2:T(8,128)S(1)}, f32[8,63,18]{1,0,2:T(8,128)}, u32[]{:S(2)}) copy-start(f32[8,63,18]{1,0,2:T(8,128)} %param.15) | copy-start | bytes 108868
  12.2 290.2 %all-gather.11.cloned.1.call-start = ((), (), s32[]{:S(2)}) async-start(), calls=%async_computation.5 | async-start | bytes 6553600 | tf_op jit(solution)/shard_map/all_gather | solution.py:95
  168.9 269.1 %reduce-scatter.3.cloned.1.call-start = ((), (), s32[]{:S(2)}) async-start(), calls=%async_computation.6 | async-start | bytes 10485760 | tf_op jit(solution)/shard_map/reduce_scatter | solution.py:130
  169.0 162.1 %copy-start.8 = (s32[8,63]{1,0:T(8,128)S(1)}, s32[8,63]{1,0:T(8,128)}, u32[]{:S(2)}) copy-start(s32[8,63]{1,0:T(8,128)} %param.16) | copy-start | bytes 6052
  169.0 162.2 %copy-start.6 = (s32[8,63]{1,0:T(8,128)S(1)}, s32[8,63]{1,0:T(8,128)}, u32[]{:S(2)}) copy-start(s32[8,63]{1,0:T(8,128)} %param.18) | copy-start | bytes 6052
  169.0 162.2 %copy-start.7 = (f32[8,63]{1,0:T(8,128)S(1)}, f32[8,63]{1,0:T(8,128)}, u32[]{:S(2)}) copy-start(f32[8,63]{1,0:T(8,128)} %param.17) | copy-start | bytes 6052
  313.3 1.1 copy-start.3
  351.7 303.3 %all-gather.15.cloned.1.call-start = ((), (), s32[]{:S(2)}) async-start(), calls=%async_computation.8 | async-start | bytes 9437184 | tf_op jit(solution)/shard_map/all_gather | solution.py:126
  363.6 132.3 %all-to-all-start = ((bf16[512,8,512]{0,2,1:T(8,128)(2,1)}), bf16[512,8,512]{0,2,1:T(8,128)(2,1)}, u32[]{:S(2)}, u32[]{:S(2)}) async-start(bf16[512,8,512]{0,2,1:T(8,128)(2,1)} %bitcast.65), calls=%async_computation | async-start | bytes 8388608 | tf_op jit(solution)/shard_map/all_to_all | solution.py:123
  368.2 321.1 %all-gather.13.cloned.1.call-start = ((), (), s32[]{:S(2)}) async-start(), calls=%async_computation.7 | async-start | bytes 9437184 | tf_op jit(solution)/shard_map/all_gather | solution.py:126
  441.3 2.2 slice-start
  495.9 159.1 %all-to-all-start.1 = ((bf16[512,8,512]{2,0,1:T(8,128)(2,1)}), bf16[512,8,512]{2,0,1:T(8,128)(2,1)}, u32[]{:S(2)}, u32[]{:S(2)}) async-start(bf16[512,8,512]{2,0,1:T(8,128)(2,1)} %bitcast.66), calls=%async_computation.2 | async-start | bytes 8388608 | tf_op jit(solution)/shard_map/all_to_all | solution.py:123
  500.5 220.0 %reduce-scatter.5.cloned.1.call-start = ((), (), s32[]{:S(2)}) async-start(), calls=%async_computation.9 | async-start | bytes 110592 | tf_op jit(solution)/shard_map/reduce_scatter | solution.py:118
  500.5 7.3 copy-start.4
  689.3 31.2 %copy-start.1 = (bf16[1024,19]{0,1:T(8,128)(2,1)S(1)}, bf16[1024,19]{0,1:T(8,128)(2,1)}, u32[]{:S(2)}) copy-start(bf16[1024,19]{0,1:T(8,128)(2,1)} %param.14) | copy-start | bytes 116740
Sparse Core Ops, SparseCore 0:
  10.4 64.0 all-gather.8
  76.1 82.0 all-gather.16
  159.7 80.5 all-gather.18
  242.6 59.7 all-gather.10
  351.8 86.1 reduce-scatter.2
  439.4 153.6 all-gather.14
  594.7 94.5 all-gather.12
  692.1 28.3 reduce-scatter.4
where the time goes:
time: 728 us; the launch traced here: 727 us
  waiting for transfers between devices  593 us (81%)
  matrix products  54.4 us (7%)
  local copies, waits for them, and re-layouts  28.9 us (4%)
  blocking collectives  16.2 us (2%)
  between operations  14.3 us (2%)
  other arithmetic  9.97 us (1%)
  starting transfers between devices  9.68 us (1%)
    all_to_all x2, waiting for transfers between devices, per_device(): lax.all_to_all(inputs_full[layer_index], 'dp', split_axis=1, concat_axis=...  196 us
    all_gather x2, waiting for transfers between devices, per_device(): lax.all_gather(trunk_weights[layer_index], 'dp', axis=0, tiled=True)  155 us
    all_gather x2, waiting for transfers between devices, per_device(): forward_whole = lax.all_gather(current, 'group', axis=1, tiled=True)  124 us
    reduce_scatter x1, waiting for transfers between devices, per_device(): lax.psum_scatter(full_grad, 'group', scatter_dimension=1, tiled=True)  69.6 us
    all_gather x2, waiting for transfers between devices, per_device(): all_upstream = lax.all_gather(pre_grad, 'dp', axis=0, tiled=True)  26 us
    dot_general x2, matrix products, per_device(): jnp.dot(forward_whole, gathered_weights[forward_layer_index], preferred_e...  21.6 us
    reduce_scatter x1, waiting for transfers between devices, per_device(): lax.psum_scatter(head_partial, 'dp', scatter_dimension=0, tiled=True)  20.5 us
    dot_general x3, matrix products, contract_rows(): lax.dot_general(left, right, (((0,), (0,)), ((), ())), preferred_element_...  17.4 us
  transfers between devices with their start and end apart: 10, of which 9 were waited for; matrix products, arithmetic and copies ran while one was open for 8% of the time, Pallas kernels for 0%

commit v1 on v0

--- a/solution.py
+++ b/solution.py
@@ -92,7 +92,15 @@
     products_block = []
     current = joined
     for forward_layer_index in range(layer_total):
-        forward_whole = lax.all_gather(current, "group", axis=1, tiled=True)
+        count_all = lax.psum(1, "group")
+        slots = [(dev, (dev + 1) % count_all) for dev in range(count_all)]
+        ready = [None] * count_all
+        ready[count_all - 1] = current
+        for kk in range(count_all - 2, -1, -1):
+            ready[kk] = lax.ppermute(ready[kk + 1], "group", slots)
+        base_arr = jnp.concatenate(ready, axis=1)
+        now = (lax.axis_index("group") + 1) * current.shape[1]
+        forward_whole = jnp.roll(base_arr, shift=now, axis=1)
         inputs_full.append(forward_whole)
         product = jnp.dot(
             forward_whole, gathered_weights[forward_layer_index], preferred_element_type=jnp.float32

time: 728 us -> 683 us (0.938)
  waiting for transfers between devices: 593 us -> 490 us
  other arithmetic: 9.97 us -> 62.3 us
    ppermute x0 -> x6, waiting for transfers between devices: none -> 177 us  [per_device(): ready[kk] = lax.ppermute(ready[kk + 1], 'group', slots)]
    all_gather x2, waiting for transfers between devices: 155 us -> 0.02 us  [per_device(): lax.all_gather(trunk_weights[layer_index], 'dp', axis=0, tiled=True)]
    all_gather x2 -> x0, waiting for transfers between devices: 124 us -> none  [per_device(): forward_whole = lax.all_gather(current, 'group', axis=1, tiled=True)]
    concatenate x0 -> x2, other arithmetic: none -> 54.8 us  [per_device(): forward_whole = jnp.roll(base_arr, shift=now, axis=1)]
  transfers between devices with their start and end apart: 10 -> 14, of which waited for: 9 -> 11; matrix products, arithmetic and copies ran while one was open for 8% -> 16% of each run, Pallas kernels for 0% -> 0%
where the time goes in v1:
time: 683 us
  waiting for transfers between devices  490 us (72%)
  other arithmetic  62.3 us (9%)
  matrix products  53.9 us (8%)
  local copies, waits for them, and re-layouts  32.4 us (5%)
  blocking collectives  14.8 us (2%)
  between operations  14.3 us (2%)
  starting transfers between devices  13.2 us (2%)
    all_to_all x2, waiting for transfers between devices, per_device(): lax.all_to_all(inputs_full[layer_index], 'dp', split_axis=1, concat_axis=...  196 us
    ppermute x6, waiting for transfers between devices, per_device(): ready[kk] = lax.ppermute(ready[kk + 1], 'group', slots)  177 us
    reduce_scatter x1, waiting for transfers between devices, per_device(): lax.psum_scatter(full_grad, 'group', scatter_dimension=1, tiled=True)  70 us
    concatenate x2, other arithmetic, per_device(): forward_whole = jnp.roll(base_arr, shift=now, axis=1)  54.8 us
    all_gather x2, waiting for transfers between devices, per_device(): all_upstream = lax.all_gather(pre_grad, 'dp', axis=0, tiled=True)  25.6 us
    dot_general x2, matrix products, per_device(): jnp.dot(forward_whole, gathered_weights[forward_layer_index], preferred_e...  21 us
    reduce_scatter x1, waiting for transfers between devices, per_device(): lax.psum_scatter(head_partial, 'dp', scatter_dimension=0, tiled=True)  20.7 us
    dot_general x3, matrix products, contract_rows(): lax.dot_general(left, right, (((0,), (0,)), ((), ())), preferred_element_...  17.4 us
  transfers between devices with their start and end apart: 14, of which 11 were waited for; matrix products, arithmetic and copies ran while one was open for 16% of the time, Pallas kernels for 0%

profile of v1, /device:TPU:0, one launch (start us, length us, event | category | flops | bytes accessed | tf_op | source)
XLA Modules:
  0.0 682.5 jit_solution(9371545643709056528)
XLA Ops:
  14.3 29.7 %collective-permute-done = bf16[640,1024]{1,0:T(8,128)(2,1)S(1)} collective-permute-done((bf16[640,1024]{1,0:T(8,128)(2,1)S(1)}, bf16[640,1024]{1,0:T(8,128)(2,1)S(1)}, u32[]{:S(2)}, u32[]{:S(2)}) %collective-permute-start) | collective-permute-done | bytes 1310752 | tf_op jit(solution)/shard_map/ppermute | solution.py:100
  44.9 30.3 %collective-permute-done.1 = bf16[640,1024]{1,0:T(8,128)(2,1)} collective-permute-done((bf16[640,1024]{1,0:T(8,128)(2,1)S(1)}, bf16[640,1024]{1,0:T(8,128)(2,1)}, u32[]{:S(2)}, u32[]{:S(2)}) %collective-permute-start.1) | collective-permute-done | bytes 1310752 | tf_op jit(solution)/shard_map/ppermute | solution.py:100
  75.1 30.4 %collective-permute-done.2 = bf16[640,1024]{1,0:T(8,128)(2,1)} collective-permute-done((bf16[640,1024]{1,0:T(8,128)(2,1)}, bf16[640,1024]{1,0:T(8,128)(2,1)}, u32[]{:S(2)}, u32[]{:S(2)}) %collective-permute-start.2) | collective-permute-done | bytes 1310752 | tf_op jit(solution)/shard_map/ppermute | solution.py:100
  105.5 44.2 %fusion.18 = bf16[640,4096]{1,0:T(8,128)(2,1)} fusion(s32[]{:T(128)S(6)} %select_n.13, bf16[640,1024]{1,0:T(8,128)(2,1)} %collective-permute-done.2, bf16[640,1024]{1,0:T(8,128)(2,1)} %collective-permute-done.1, bf16[640,1024]{1,0:T(8,128)(2,1)S(1)} %collective-permute-done, bf16[512,1024]{1,0:T(8,128)(2,1)S(1)} %bitcast.70, bf16[128,1024]{1,0:T(8,128)(2,1)S(1)} %copy-done.7), kind=kLoop, calls=%fused_computation.37 | loop fusion | flops 52428800 | bytes 10485764 | tf_op jit(solution)/shard_map/jit(_roll_dynamic)/concatenate | solution.py:103
  149.7 10.1 %multiply_convert_fusion.1 = (bf16[640,1024]{1,0:T(8,128)(2,1)S(1)}, f32[640,1024]{1,0:T(8,128)S(1)}) fusion(bf16[640,4096]{1,0:T(8,128)(2,1)} %fusion.18, bf16[1,4096,1024]{2,1,0:T(8,128)(2,1)} %all-gather.11.cloned.1.call-done), kind=kOutput, calls=%fused_computation.46 | convolution fusion | flops 5371985920 | bytes 17563648 | tf_op jit(solution)/shard_map/dot_general | solution.py:105
  161.0 29.4 %collective-permute-done.3 = bf16[640,1024]{1,0:T(8,128)(2,1)S(1)} collective-permute-done((bf16[640,1024]{1,0:T(8,128)(2,1)S(1)}, bf16[640,1024]{1,0:T(8,128)(2,1)S(1)}, u32[]{:S(2)}, u32[]{:S(2)}) %collective-permute-start.3) | collective-permute-done | bytes 1310752 | tf_op jit(solution)/shard_map/ppermute | solution.py:100
  191.5 28.7 %collective-permute-done.4 = bf16[640,1024]{1,0:T(8,128)(2,1)} collective-permute-done((bf16[640,1024]{1,0:T(8,128)(2,1)S(1)}, bf16[640,1024]{1,0:T(8,128)(2,1)}, u32[]{:S(2)}, u32[]{:S(2)}) %collective-permute-start.4) | collective-permute-done | bytes 1310752 | tf_op jit(solution)/shard_map/ppermute | solution.py:100
  220.3 28.0 %collective-permute-done.5 = bf16[640,1024]{1,0:T(8,128)(2,1)} collective-permute-done((bf16[640,1024]{1,0:T(8,128)(2,1)}, bf16[640,1024]{1,0:T(8,128)(2,1)}, u32[]{:S(2)}, u32[]{:S(2)}) %collective-permute-start.5) | collective-permute-done | bytes 1310752 | tf_op jit(solution)/shard_map/ppermute | solution.py:100
  248.2 10.6 %fusion.11 = bf16[640,4096]{1,0:T(8,128)(2,1)} fusion(s32[]{:T(128)S(6)} %select_n.13, bf16[640,1024]{1,0:T(8,128)(2,1)} %collective-permute-done.5, bf16[640,1024]{1,0:T(8,128)(2,1)} %collective-permute-done.4, bf16[640,1024]{1,0:T(8,128)(2,1)} %copy-done.6, bf16[640,1024]{1,0:T(8,128)(2,1)} %copy-done.5), kind=kLoop, calls=%fused_computation.30 | loop fusion | flops 41943040 | bytes 10485764 | tf_op jit(solution)/shard_map/jit(_roll_dynamic)/concatenate | solution.py:103
  258.9 10.9 %multiply_convert_fusion = (bf16[640,1024]{1,0:T(8,128)(2,1)S(1)}, f32[640,1024]{1,0:T(8,128)}) fusion(bf16[640,4096]{1,0:T(8,128)(2,1)} %fusion.11, bf16[1,4096,1024]{2,1,0:T(8,128)(2,1)} %all-gather.13.cloned.1.call-done), kind=kOutput, calls=%fused_computation.45 | convolution fusion | flops 5371985920 | bytes 17563648 | tf_op jit(solution)/shard_map/dot_general | solution.py:105
  271.3 14.8 %psum.7 = f32[640,19]{0,1:T(8,128)S(1)} all-reduce(f32[640,19]{0,1:T(8,128)S(1)} %fusion.44), channel_id=1, replica_groups=mesh['group'=4,'dp'=8] {'group'}, use_global_device_ids=true, to_apply=%region_0.2 | all-reduce | flops 12160 | bytes 97280 | tf_op jit(solution)/shard_map/psum | solution.py:111
  286.7 4.7 while.17
  295.3 11.5 %fusion.2 = f32[512,4096]{1,0:T(8,128)} fusion(bf16[512,1024]{1,0:T(8,128)(2,1)} %multiply_convert_fusion.3, bf16[1,4096,1024]{2,1,0:T(8,128)(2,1)} %all-gather.13.cloned.1.call-done), kind=kOutput, calls=%fused_computation.21 | convolution fusion | flops 4294967296 | bytes 17825792 | tf_op jit(solution)/shard_map/dot_general | solution.py:19
  307.4 4.7 slice.62
  312.1 6.6 copy.47
  323.3 70.0 %reduce-scatter.3.cloned.1.call-done = f32[512,1024]{1,0:T(8,128)} async-done(((f32[512,4096]{1,0:T(8,128)}), f32[512,1024]{1,0:T(8,128)}) %reduce-scatter.3.cloned.1.call-update) | async-done | bytes 2097168 | tf_op jit(solution)/shard_map/reduce_scatter | solution.py:138
  401.3 49.2 %all-to-all-done = bf16[512,8,512]{0,2,1:T(8,128)(2,1)} async-done(((bf16[512,8,512]{0,2,1:T(8,128)(2,1)}), bf16[512,8,512]{0,2,1:T(8,128)(2,1)}, u32[]{:S(2)}, u32[]{:S(2)}) %all-to-all-start) | async-done | bytes 4194336 | tf_op jit(solution)/shard_map/all_to_all | solution.py:131
  450.5 4.6 all-to-all-start.1
  455.2 6.5 copy.48
  463.2 147.1 %all-to-all-done.1 = bf16[512,8,512]{2,0,1:T(8,128)(2,1)} async-done(((bf16[512,8,512]{2,0,1:T(8,128)(2,1)}), bf16[512,8,512]{2,0,1:T(8,128)(2,1)}, u32[]{:S(2)}, u32[]{:S(2)}) %all-to-all-start.1) | async-done | bytes 4194336 | tf_op jit(solution)/shard_map/all_to_all | solution.py:131
  610.3 8.3 %convolution_bitcast_fusion = f32[1,512,1024]{2,1,0:T(8,128)S(1)} fusion(bf16[4096,512]{1,0:T(8,128)(2,1)} %bitcast.13, bf16[4096,1024]{1,0:T(8,128)(2,1)} %all-gather.9.cloned.1.call-done), kind=kOutput, calls=%fused_computation.49 | convolution fusion | flops 4294967296 | bytes 14680064 | tf_op jit(solution)/shard_map/dot_general | solution.py:13
  618.7 25.6 %all-gather.7.cloned.1.call-done = bf16[4096,1024]{1,0:T(8,128)(2,1)} async-done(((bf16[512,1024]{1,0:T(8,128)(2,1)}), bf16[4096,1024]{1,0:T(8,128)(2,1)}) %all-gather.7.cloned.1.call-update) | async-done | bytes 8388624 | tf_op jit(solution)/shard_map/all_gather | solution.py:134
  644.3 8.2 %convolution_bitcast_fusion.1 = f32[1,512,1024]{2,1,0:T(8,128)S(1)} fusion(bf16[4096,512]{1,0:T(8,128)(2,1)} %bitcast.68, bf16[4096,1024]{1,0:T(8,128)(2,1)} %all-gather.7.cloned.1.call-done), kind=kOutput, calls=%fused_computation.50 | convolution fusion | flops 4294967296 | bytes 14680064 | tf_op jit(solution)/shard_map/dot_general | solution.py:13
  655.0 20.7 %reduce-scatter.5.cloned.1.call-done = f32[128,19]{0,1:T(8,128)} async-done(((f32[1024,19]{0,1:T(8,128)}), f32[128,19]{0,1:T(8,128)}) %reduce-scatter.5.cloned.1.call-update) | async-done | bytes 9744 | tf_op jit(solution)/shard_map/reduce_scatter | solution.py:126
  (207 shorter events, 36.9 us)
Async XLA Ops:
  7.2 263.7 %copy-start = (bf16[1024,19]{0,1:T(8,128)(2,1)S(1)}, bf16[1024,19]{0,1:T(8,128)(2,1)}, u32[]{:S(2)}) copy-start(bf16[1024,19]{0,1:T(8,128)(2,1)} %param.16) | copy-start | bytes 116740
  7.2 4.0 copy-start.7
  7.2 4.0 copy-start.2
  7.2 142.5 %all-gather.11.cloned.1.call-start = ((), (), s32[]{:S(2)}) async-start(), calls=%async_computation.8 | async-start | bytes 9437184 | tf_op jit(solution)/shard_map/all_gather | solution.py:87
  10.4 248.5 %all-gather.13.cloned.1.call-start = ((), (), s32[]{:S(2)}) async-start(), calls=%async_computation.9 | async-start | bytes 9437184 | tf_op jit(solution)/shard_map/all_gather | solution.py:87
  11.1 382.2 %reduce-scatter.3.cloned.1.call-start = ((), (), s32[]{:S(2)}) async-start(), calls=%async_computation.4 | async-start | bytes 10485760 | tf_op jit(solution)/shard_map/reduce_scatter | solution.py:138
  11.3 32.8 %collective-permute-start = (bf16[640,1024]{1,0:T(8,128)(2,1)S(1)}, bf16[640,1024]{1,0:T(8,128)(2,1)S(1)}, u32[]{:S(2)}, u32[]{:S(2)}) collective-permute-start(bf16[640,1024]{1,0:T(8,128)(2,1)S(1)} %pad_maximum_fusion.1), channel_id=1, source_target_pairs={{0,8},{8,16},{16,24},{24,0},{1,9},{9,17},{17,25},{25,1},{2,10},{10... | collective-permute-start | bytes 3932168 | tf_op jit(solution)/shard_map/ppermute | solution.py:100
  44.1 31.1 %collective-permute-start.1 = (bf16[640,1024]{1,0:T(8,128)(2,1)S(1)}, bf16[640,1024]{1,0:T(8,128)(2,1)}, u32[]{:S(2)}, u32[]{:S(2)}) collective-permute-start(bf16[640,1024]{1,0:T(8,128)(2,1)S(1)} %collective-permute-done), channel_id=1, source_target_pairs={{0,8},{8,16},{16,24},{24,0},{1,9},{9,17},{17,25},{25,1},{2,10},{10... | collective-permute-start | bytes 3932168 | tf_op jit(solution)/shard_map/ppermute | solution.py:100
  75.1 30.4 %collective-permute-start.2 = (bf16[640,1024]{1,0:T(8,128)(2,1)}, bf16[640,1024]{1,0:T(8,128)(2,1)}, u32[]{:S(2)}, u32[]{:S(2)}) collective-permute-start(bf16[640,1024]{1,0:T(8,128)(2,1)} %collective-permute-done.1), channel_id=1, source_target_pairs={{0,8},{8,16},{16,24},{24,0},{1,9},{9,17},{17,25},{25,1},{2,10},{10... | collective-permute-start | bytes 3932168 | tf_op jit(solution)/shard_map/ppermute | solution.py:100
  149.7 70.5 %copy-start.8 = (f32[8,63,18]{1,0,2:T(8,128)S(1)}, f32[8,63,18]{1,0,2:T(8,128)}, u32[]{:S(2)}) copy-start(f32[8,63,18]{1,0,2:T(8,128)} %param.17) | copy-start | bytes 108868
  161.0 29.4 %collective-permute-start.3 = (bf16[640,1024]{1,0:T(8,128)(2,1)S(1)}, bf16[640,1024]{1,0:T(8,128)(2,1)S(1)}, u32[]{:S(2)}, u32[]{:S(2)}) collective-permute-start(bf16[640,1024]{1,0:T(8,128)(2,1)S(1)} %get-tuple-element.150), channel_id=1, source_target_pairs={{0,8},{8,16},{16,24},{24,0},{1,9},{9,17},{17,25},{25,1},{2,10},{10... | collective-permute-start | bytes 3932168 | tf_op jit(solution)/shard_map/ppermute | solution.py:100
  191.5 28.7 %collective-permute-start.4 = (bf16[640,1024]{1,0:T(8,128)(2,1)S(1)}, bf16[640,1024]{1,0:T(8,128)(2,1)}, u32[]{:S(2)}, u32[]{:S(2)}) collective-permute-start(bf16[640,1024]{1,0:T(8,128)(2,1)S(1)} %collective-permute-done.3), channel_id=1, source_target_pairs={{0,8},{8,16},{16,24},{24,0},{1,9},{9,17},{17,25},{25,1},{2,10},{10... | collective-permute-start | bytes 3932168 | tf_op jit(solution)/shard_map/ppermute | solution.py:100
  220.2 28.0 %collective-permute-start.5 = (bf16[640,1024]{1,0:T(8,128)(2,1)}, bf16[640,1024]{1,0:T(8,128)(2,1)}, u32[]{:S(2)}, u32[]{:S(2)}) collective-permute-start(bf16[640,1024]{1,0:T(8,128)(2,1)} %collective-permute-done.4), channel_id=1, source_target_pairs={{0,8},{8,16},{16,24},{24,0},{1,9},{9,17},{17,25},{25,1},{2,10},{10... | collective-permute-start | bytes 3932168 | tf_op jit(solution)/shard_map/ppermute | solution.py:100
  258.9 27.4 %copy-start.11 = (s32[8,63]{1,0:T(8,128)S(1)}, s32[8,63]{1,0:T(8,128)}, u32[]{:S(2)}) copy-start(s32[8,63]{1,0:T(8,128)} %param.18) | copy-start | bytes 6052
  258.9 27.6 %copy-start.9 = (s32[8,63]{1,0:T(8,128)S(1)}, s32[8,63]{1,0:T(8,128)}, u32[]{:S(2)}) copy-start(s32[8,63]{1,0:T(8,128)} %param.20) | copy-start | bytes 6052
  258.9 27.6 %copy-start.10 = (f32[8,63]{1,0:T(8,128)S(1)}, f32[8,63]{1,0:T(8,128)}, u32[]{:S(2)}) copy-start(f32[8,63]{1,0:T(8,128)} %param.19) | copy-start | bytes 6052
  306.9 303.5 %all-gather.9.cloned.1.call-start = ((), (), s32[]{:S(2)}) async-start(), calls=%async_computation.6 | async-start | bytes 9437184 | tf_op jit(solution)/shard_map/all_gather | solution.py:134
  318.7 131.8 %all-to-all-start = ((bf16[512,8,512]{0,2,1:T(8,128)(2,1)}), bf16[512,8,512]{0,2,1:T(8,128)(2,1)}, u32[]{:S(2)}, u32[]{:S(2)}) async-start(bf16[512,8,512]{0,2,1:T(8,128)(2,1)} %bitcast.66), calls=%async_computation | async-start | bytes 8388608 | tf_op jit(solution)/shard_map/all_to_all | solution.py:131
  323.3 321.0 %all-gather.7.cloned.1.call-start = ((), (), s32[]{:S(2)}) async-start(), calls=%async_computation.5 | async-start | bytes 9437184 | tf_op jit(solution)/shard_map/all_gather | solution.py:134
  396.7 2.2 slice-start
  450.5 159.8 %all-to-all-start.1 = ((bf16[512,8,512]{2,0,1:T(8,128)(2,1)}), bf16[512,8,512]{2,0,1:T(8,128)(2,1)}, u32[]{:S(2)}, u32[]{:S(2)}) async-start(bf16[512,8,512]{2,0,1:T(8,128)(2,1)} %bitcast.67), calls=%async_computation.2 | async-start | bytes 8388608 | tf_op jit(solution)/shard_map/all_to_all | solution.py:131
  455.1 7.2 %copy-start.4 = (bf16[640,1024]{1,0:T(8,128)(2,1)S(1)}, bf16[640,1024]{1,0:T(8,128)(2,1)}, u32[]{:S(2)}) copy-start(bf16[640,1024]{1,0:T(8,128)(2,1)} %copy-done.3) | copy-start | bytes 3932164
  455.1 220.6 %reduce-scatter.5.cloned.1.call-start = ((), (), s32[]{:S(2)}) async-start(), calls=%async_computation.7 | async-start | bytes 110592 | tf_op jit(solution)/shard_map/reduce_scatter | solution.py:126
  644.3 31.4 %copy-start.1 = (bf16[1024,19]{0,1:T(8,128)(2,1)S(1)}, bf16[1024,19]{0,1:T(8,128)(2,1)}, u32[]{:S(2)}) copy-start(bf16[1024,19]{0,1:T(8,128)(2,1)} %param.16) | copy-start | bytes 116740
  (3 other events, 3.2 us)
Sparse Core Ops, SparseCore 0:
  10.5 84.7 all-gather.10
  96.9 80.5 all-gather.12
  307.0 86.2 reduce-scatter.2
  394.8 153.5 all-gather.8
  549.8 94.4 all-gather.6
  647.0 28.6 reduce-scatter.4
